TPU v7x, 32 devices: a 4x4x1 block of a 4x4x8 slice. The times are simulated.
32 devices in a mesh: dp: 1 (over z), ey: 4 (over y), ex: 4 (over x), core: 2 (over core).
Axes of the slice: x: 4, y: 4, z: 1, core: 2. Of those that a mesh axis runs over, the one named last changes fastest.
The devices are a block of a 4x4x8 slice.
Arguments:
- tokens: bfloat16 [24576, 2048], P(('dp', 'ey', 'ex', 'core'))
- expert_ids: int32 [24576, 8], P(('dp', 'ey', 'ex', 'core'))
- gate_prob: float32 [24576, 8], P(('dp', 'ey', 'ex', 'core'))
- w_gate: bfloat16 [64, 2048, 1024], P(('ey', 'ex', 'core'))
- w_up: bfloat16 [64, 2048, 1024], P(('ey', 'ex', 'core'))
- w_down: bfloat16 [64, 1024, 2048], P(('ey', 'ex', 'core'))
Outputs:
- output: bfloat16 [24576, 2048], P(('dp', 'ey', 'ex', 'core'))
All inputs are finite; a program needn't handle non-finite values.
Results may differ from a plain program's by a relative error of at most 0.0116772.
Values are sent between devices in bfloat16 or wider.
A program may use at most 768 MiB of HBM per device.

v0:
```python
import jax
import jax.numpy as jnp
from jax import lax
from jax.sharding import PartitionSpec as P

GROUP_AXES = ('ey', 'ex', 'core')
TOKEN_SPEC = P(('dp', 'ey', 'ex', 'core'), None)
EXPERT_SPEC = P(('ey', 'ex', 'core'), None, None)


def target_chips(grid_y, grid_x):
    half_y = grid_y // 2
    half_x = grid_x // 2
    chip_list = []
    for chip_y in range(grid_y):
        for chip_x in range(grid_x):
            if chip_y == 0 and chip_x < half_x:
                chip_list.append(half_y * grid_x + chip_x + half_x)
            elif chip_y == half_y and chip_x >= half_x:
                chip_list.append(chip_x - half_x)
            else:
                chip_list.append(chip_y * grid_x + chip_x)
    return chip_list


def extra_perms(chip_list, n_core):
    same_core = [(chip_id * n_core + core_id, chip_list[chip_id] * n_core + core_id) for chip_id in range(len(chip_list)) for core_id in range(n_core)]
    other_core = [(chip_id * n_core + core_id, chip_list[chip_id] * n_core + (core_id + 1) % n_core) for chip_id in range(len(chip_list)) for core_id in range(n_core)]
    return same_core, other_core


def reverse_pairs(pair_list):
    return [(pair_dst, pair_src) for pair_src, pair_dst in pair_list]


def expert_ffn(rows_in, w_gate, w_up, w_down):
    gate_act = jnp.einsum('sepd,edf->sepf', rows_in, w_gate, preferred_element_type=jnp.float32)
    up_act = jnp.einsum('sepd,edf->sepf', rows_in, w_up, preferred_element_type=jnp.float32)
    hidden = (jax.nn.silu(gate_act) * up_act).astype(jnp.bfloat16)
    return jnp.einsum('sepf,efd->sepd', hidden, w_down, preferred_element_type=jnp.float32).astype(jnp.bfloat16)


def copy_layout(dst_chip, core_id, n_exp, exp_dev, n_core, base_rows, hot_rows):
    hot_lo = dst_chip * n_core * exp_dev

    def sorted_start(exp_id):
        return base_rows * exp_id + hot_rows * jnp.clip(exp_id - hot_lo, 0, n_core * exp_dev)

    pos_base = sorted_start(jnp.arange(n_exp))[:, None] + jnp.arange(base_rows)[None, :]
    tgt_dev = dst_chip * n_core + (core_id + jnp.arange(n_core)) % n_core
    hot_exp = tgt_dev[:, None] * exp_dev + jnp.arange(exp_dev)[None, :]
    pos_hot = sorted_start(hot_exp)[:, :, None] + base_rows + jnp.arange(hot_rows)[None, None, :]
    return jnp.concatenate([pos_base.reshape(-1), pos_hot.reshape(-1)])


def solution(mesh):
    grid_y = mesh.shape['ey']
    grid_x = mesh.shape['ex']
    n_core = mesh.shape['core']
    n_dev = grid_y * grid_x * n_core
    chip_list = target_chips(grid_y, grid_x)
    perm_same, perm_other = extra_perms(chip_list, n_core)
    back_same = reverse_pairs(perm_same)
    back_other = reverse_pairs(perm_other)

    def device_body(tokens, expert_ids, gate_prob, w_gate, w_up, w_down):
        tok_dev, top_k = expert_ids.shape
        d_model = tokens.shape[1]
        exp_dev = w_gate.shape[0]
        n_exp = exp_dev * n_dev
        n_copy = tok_dev * top_k
        base_rows = 2 * n_copy // (3 * n_exp)
        hot_rows = grid_y * grid_x * base_rows // 2
        n_base = n_exp * base_rows
        core_id = lax.axis_index('core')
        chip_id = lax.axis_index('ey') * grid_x + lax.axis_index('ex')
        dst_chip = jnp.asarray(chip_list, dtype=jnp.int32)[chip_id]
        sort_order = jnp.argsort(expert_ids.reshape(n_copy), stable=True)
        src_copy = sort_order[copy_layout(dst_chip, core_id, n_exp, exp_dev, n_core, base_rows, hot_rows)]
        send_rows = tokens[src_copy // top_k]
        send_base = send_rows[:n_base].reshape(n_dev, exp_dev, base_rows, d_model)
        send_hot = send_rows[n_base:].reshape(n_core, 1, exp_dev, hot_rows, d_model)
        recv_base = lax.all_to_all(send_base, GROUP_AXES, 0, 0, tiled=True)
        recv_same = lax.ppermute(send_hot[0], GROUP_AXES, perm_same)
        recv_other = lax.ppermute(send_hot[1], GROUP_AXES, perm_other)
        y_base = expert_ffn(recv_base, w_gate, w_up, w_down)
        y_same = expert_ffn(recv_same, w_gate, w_up, w_down)
        y_other = expert_ffn(recv_other, w_gate, w_up, w_down)
        ret_base = lax.all_to_all(y_base, GROUP_AXES, 0, 0, tiled=True)
        ret_same = lax.ppermute(y_same, GROUP_AXES, back_same)
        ret_other = lax.ppermute(y_other, GROUP_AXES, back_other)
        y_rows = jnp.concatenate([ret_base.reshape(n_base, d_model), ret_same.reshape(-1, d_model), ret_other.reshape(-1, d_model)])
        y_copy = y_rows[jnp.argsort(src_copy)].reshape(tok_dev, top_k, d_model)
        mixed_out = jnp.sum(y_copy.astype(jnp.float32) * gate_prob[:, :, None], axis=1)
        return mixed_out.astype(jnp.bfloat16)

    return jax.shard_map(device_body, mesh=mesh, in_specs=(TOKEN_SPEC, TOKEN_SPEC, TOKEN_SPEC, EXPERT_SPEC, EXPERT_SPEC, EXPERT_SPEC), out_specs=TOKEN_SPEC, check_vma=False)
```

profile of v0, /device:TPU:98, one launch (start us, length us, event | category | flops | bytes accessed | tf_op | source)
XLA Modules:
  0.0 1019.0 jit_solution(15874520757918565166)
XLA Ops:
  0.0 0.0 copy-start
  0.0 1.0 copy.13
  1.1 0.8 reshape.267
  1.9 1.2 dynamic_slice.3
  3.7 0.1 iota_add_fusion
  3.7 0.1 concatenate.29
  4.4 0.1 add_add_fusion
  4.5 0.1 iota_add_fusion.1
  4.7 7.4 sort.34
  12.1 34.3 %gather_fusion = s32[6144]{0:T(1024)S(1)} fusion(s32[6144]{0:T(1024)S(1)} %get-tuple-element.7, s32[6144]{0:T(1024)S(1)} %broadcast_clamp_fusion.1), kind=kCustom, calls=%fused_computation | custom fusion | bytes 73728 | tf_op jit(solution)/shard_map/gather | solution.py:79
  46.4 0.0 copy-start.2
  46.4 0.1 compare_select_fusion
  46.6 0.0 copy-done
  46.6 30.9 %gather_fusion.1 = bf16[6144,2048]{1,0:T(8,128)(2,1)} fusion(bf16[768,2048]{1,0:T(8,128)(2,1)S(1)} %copy-done, s32[6144]{0:T(1024)S(1)} %broadcast_clamp_fusion), kind=kCustom, calls=%fused_computation.1 | custom fusion | bytes 50356224 | tf_op jit(solution)/shard_map/gather | solution.py:80
  77.5 0.0 copy-done.2
  77.5 14.1 %slice.23 = bf16[4096,2048]{1,0:T(8,128)(2,1)} slice(bf16[6144,2048]{1,0:T(8,128)(2,1)} %gather_fusion.1), slice={[0:4096], [0:2048]} | slice | bytes 33554432 | tf_op jit(solution)/shard_map/slice | solution.py:81
  91.6 8.7 all-to-all-start
  100.3 6.0 fusion.56
  106.4 4.3 collective-permute-start.2
  110.7 210.3 %all-to-all-done = bf16[32,2,64,2048]{3,2,1,0:T(8,128)(2,1)} async-done(((bf16[32,2,64,2048]{3,2,1,0:T(8,128)(2,1)}), bf16[32,2,64,2048]{3,2,1,0:T(8,128)(2,1)}, u32[]{:S(2)}, u32[]{:S(2)}) %all-to-all-start) | async-done | bytes 16777248 | tf_op jit(solution)/shard_map/all_to_all | solution.py:83
  321.0 24.6 %fusion.5 = f32[2,32,64,1024]{3,2,1,0:T(8,128)} fusion(bf16[32,2,64,2048]{3,2,1,0:T(8,128)(2,1)} %all-to-all-done, bf16[2,2048,1024]{2,1,0:T(8,128)(2,1)} %param.11), kind=kOutput, calls=%fused_computation.14 | convolution fusion | flops 17179869184 | bytes 41943040 | tf_op jit(solution)/shard_map/sepd,edf->sepf/dot_general | solution.py:38
  345.6 44.8 %convert_bitcast_fusion = bf16[32,2,64,2048]{3,2,0,1:T(8,128)(2,1)} fusion(f32[2,32,64,1024]{3,2,1,0:T(8,128)} %fusion.5, bf16[32,2,64,2048]{3,2,1,0:T(8,128)(2,1)} %all-to-all-done, bf16[2,1024,2048]{2,1,0:T(8,128)(2,1)} %param.12, bf16[2,2048,1024]{2,1,0:T(8,128)(2,1)} %param.10), kind=kOutput, calls=%fused_computation.13 | convolution fusion | flops 34393292800 | bytes 67108864 | tf_op jit(solution)/shard_map/sepf,efd->sepd/dot_general | solution.py:40
  390.4 14.1 %copy.16 = bf16[32,2,64,2048]{3,2,1,0:T(8,128)(2,1)} copy(bf16[32,2,64,2048]{3,2,0,1:T(8,128)(2,1)} %convert_bitcast_fusion) | data formatting | bytes 33554432 | tf_op jit(solution)/shard_map/convert_element_type | solution.py:40
  404.5 12.1 %all-to-all-start.1 = ((bf16[32,2,64,2048]{3,2,1,0:T(8,128)(2,1)}), bf16[32,2,64,2048]{3,2,1,0:T(8,128)(2,1)}, u32[]{:S(2)}, u32[]{:S(2)}) async-start(bf16[32,2,64,2048]{3,2,1,0:T(8,128)(2,1)} %copy.16), calls=%async_computation.1 | async-start | bytes 33554432 | tf_op jit(solution)/shard_map/all_to_all | solution.py:89
  416.6 6.7 collective-permute-start
  423.3 0.0 collective-permute-done.2
  423.3 11.1 %fusion.26 = f32[2,512,1024]{2,1,0:T(8,128)} fusion(bf16[2,2048,1024]{2,1,0:T(8,128)(2,1)} %param.10, bf16[1,2,512,2048]{3,2,1,0:T(8,128)(2,1)} %collective-permute-done.2), kind=kOutput, calls=%fused_computation.33 | convolution fusion | flops 4294967296 | bytes 16777216 | tf_op jit(solution)/shard_map/sepd,edf->sepf/dot_general | solution.py:37
  434.4 15.2 %convert_bitcast_fusion.1 = bf16[1,2,512,2048]{3,2,1,0:T(8,128)(2,1)} fusion(bf16[2,1024,2048]{2,1,0:T(8,128)(2,1)} %param.12, f32[2,512,1024]{2,1,0:T(8,128)} %fusion.26, bf16[2,2048,1024]{2,1,0:T(8,128)(2,1)} %param.11, bf16[1,2,512,2048]{3,2,1,0:T(8,128)(2,1)} %collective-permute-done.2), kind=kOutput, calls=%fused_computation.44 | convolution fusion | flops 8598323200 | bytes 29360128 | tf_op jit(solution)/shard_map/sepf,efd->sepd/dot_general | solution.py:40
  449.5 0.8 collective-permute-start.3
  450.4 286.8 %collective-permute-done = bf16[1,2,512,2048]{3,2,1,0:T(8,128)(2,1)} collective-permute-done((bf16[1,2,512,2048]{3,2,1,0:T(8,128)(2,1)}, bf16[1,2,512,2048]{3,2,1,0:T(8,128)(2,1)}, u32[]{:S(2)}, u32[]{:S(2)}) %collective-permute-start) | collective-permute-done | bytes 4194336 | tf_op jit(solution)/shard_map/ppermute | solution.py:84
  737.1 11.2 %fusion.33 = f32[2,512,1024]{2,1,0:T(8,128)} fusion(bf16[2,2048,1024]{2,1,0:T(8,128)(2,1)} %param.10, bf16[1,2,512,2048]{3,2,1,0:T(8,128)(2,1)} %collective-permute-done), kind=kOutput, calls=%fused_computation.42 | convolution fusion | flops 4294967296 | bytes 16777216 | tf_op jit(solution)/shard_map/sepd,edf->sepf/dot_general | solution.py:37
  748.3 0.0 copy-start.3
  748.3 0.0 copy-start.4
  748.3 15.1 %convert_bitcast_fusion.2 = bf16[1,2,512,2048]{3,2,1,0:T(8,128)(2,1)} fusion(bf16[2,1024,2048]{2,1,0:T(8,128)(2,1)} %param.12, f32[2,512,1024]{2,1,0:T(8,128)} %fusion.33, bf16[2,2048,1024]{2,1,0:T(8,128)(2,1)} %param.11, bf16[1,2,512,2048]{3,2,1,0:T(8,128)(2,1)} %collective-permute-done), kind=kOutput, calls=%fused_computation.45 | convolution fusion | flops 8598323200 | bytes 29360128 | tf_op jit(solution)/shard_map/sepf,efd->sepd/dot_general | solution.py:40
  763.5 2.2 collective-permute-start.1
  765.7 0.0 copy-done.3
  765.7 6.7 sort.35
  772.4 0.0 copy-done.4
  772.4 0.2 copy.17
  772.6 0.6 fusion.49
  773.2 42.1 %collective-permute-done.3 = bf16[1,2,512,2048]{3,2,1,0:T(8,128)(2,1)} collective-permute-done((bf16[1,2,512,2048]{3,2,1,0:T(8,128)(2,1)}, bf16[1,2,512,2048]{3,2,1,0:T(8,128)(2,1)}, u32[]{:S(2)}, u32[]{:S(2)}) %collective-permute-start.3) | collective-permute-done | bytes 4194336 | tf_op jit(solution)/shard_map/ppermute | solution.py:91
  815.4 96.4 %collective-permute-done.1 = bf16[1,2,512,2048]{3,2,1,0:T(8,128)(2,1)} collective-permute-done((bf16[1,2,512,2048]{3,2,1,0:T(8,128)(2,1)}, bf16[1,2,512,2048]{3,2,1,0:T(8,128)(2,1)}, u32[]{:S(2)}, u32[]{:S(2)}) %collective-permute-start.1) | collective-permute-done | bytes 4194336 | tf_op jit(solution)/shard_map/ppermute | solution.py:90
  911.8 0.0 all-to-all-done.1
  911.8 25.3 %pad_maximum_fusion = bf16[6144,2048]{1,0:T(8,128)(2,1)} fusion(bf16[1024,2048]{1,0:T(8,128)(2,1)} %bitcast.45, bf16[1024,2048]{1,0:T(8,128)(2,1)} %bitcast.30, bf16[4096,2048]{1,0:T(8,128)(2,1)} %bitcast.15), kind=kLoop, calls=%fused_computation.5 | loop fusion | flops 75497472 | bytes 50331648 | tf_op jit(solution)/shard_map/concatenate | solution.py:92
  937.1 0.0 copy-start.1
  937.1 58.0 %gather_fusion.2 = bf16[6144,2048]{1,0:T(8,128)(2,1)} fusion(bf16[6144,2048]{1,0:T(8,128)(2,1)} %pad_maximum_fusion, s32[6144]{0:T(1024)} %fusion.49), kind=kCustom, calls=%fused_computation.2 | custom fusion | bytes 50356224 | tf_op jit(solution)/shard_map/gather | solution.py:93
  995.1 23.5 %fusion = bf16[768,2048]{1,0:T(8,128)(2,1)} fusion(bf16[6144,2048]{1,0:T(8,128)(2,1)} %gather_fusion.2, f32[768,8]{1,0:T(8,128)S(1)} %copy.17), kind=kLoop, calls=%fused_computation.4 | loop fusion | flops 36175872 | bytes 28336128 | tf_op jit(solution)/shard_map/reduce_sum | solution.py:94
  1018.5 0.0 copy-done.1
  (10 shorter events, 0.1 us)
Async XLA Ops:
  0.0 46.6 %copy-start = (bf16[768,2048]{1,0:T(8,128)(2,1)S(1)}, bf16[768,2048]{1,0:T(8,128)(2,1)}, u32[]{:S(2)}) copy-start(bf16[768,2048]{1,0:T(8,128)(2,1)} %param.7) | copy-start | bytes 9437188
  46.4 31.1 %copy-start.2 = (s32[6144]{0:T(1024)}, s32[6144]{0:T(1024)S(1)}, u32[]{:S(2)}) copy-start(s32[6144]{0:T(1024)S(1)} %gather_fusion) | copy-start | bytes 73732
  91.6 229.3 %all-to-all-start = ((bf16[32,2,64,2048]{3,2,1,0:T(8,128)(2,1)}), bf16[32,2,64,2048]{3,2,1,0:T(8,128)(2,1)}, u32[]{:S(2)}, u32[]{:S(2)}) async-start(bf16[32,2,64,2048]{3,2,1,0:T(8,128)(2,1)} %bitcast.171), calls=%async_computation | async-start | bytes 33554432 | tf_op jit(solution)/shard_map/all_to_all | solution.py:83
  106.4 317.0 %collective-permute-start.2 = (bf16[1,2,512,2048]{3,2,1,0:T(8,128)(2,1)}, bf16[1,2,512,2048]{3,2,1,0:T(8,128)(2,1)}, u32[]{:S(2)}, u32[]{:S(2)}) collective-permute-start(bf16[1,2,512,2048]{3,2,1,0:T(8,128)(2,1)} %bitcast.31), channel_id=1, source_target_pairs={{0,21},{1,20},{2,23},{3,22},{4,5},{5,4},{6,7},{7,6},{8,9},{9,8},{1... | collective-permute-start | bytes 12582920 | tf_op jit(solution)/shard_map/ppermute | solution.py:85
  404.5 507.3 %all-to-all-start.1 = ((bf16[32,2,64,2048]{3,2,1,0:T(8,128)(2,1)}), bf16[32,2,64,2048]{3,2,1,0:T(8,128)(2,1)}, u32[]{:S(2)}, u32[]{:S(2)}) async-start(bf16[32,2,64,2048]{3,2,1,0:T(8,128)(2,1)} %copy.16), calls=%async_computation.1 | async-start | bytes 33554432 | tf_op jit(solution)/shard_map/all_to_all | solution.py:89
  416.6 320.6 %collective-permute-start = (bf16[1,2,512,2048]{3,2,1,0:T(8,128)(2,1)}, bf16[1,2,512,2048]{3,2,1,0:T(8,128)(2,1)}, u32[]{:S(2)}, u32[]{:S(2)}) collective-permute-start(bf16[1,2,512,2048]{3,2,1,0:T(8,128)(2,1)} %bitcast.172), channel_id=1, source_target_pairs={{0,20},{1,21},{2,22},{3,23},{4,4},{5,5},{6,6},{7,7},{8,8},{9,9},{1... | collective-permute-start | bytes 12582920 | tf_op jit(solution)/shard_map/ppermute | solution.py:84
  449.5 365.8 %collective-permute-start.3 = (bf16[1,2,512,2048]{3,2,1,0:T(8,128)(2,1)}, bf16[1,2,512,2048]{3,2,1,0:T(8,128)(2,1)}, u32[]{:S(2)}, u32[]{:S(2)}) collective-permute-start(bf16[1,2,512,2048]{3,2,1,0:T(8,128)(2,1)} %convert_bitcast_fusion.1), channel_id=1, source_target_pairs={{21,0},{20,1},{23,2},{22,3},{5,4},{4,5},{7,6},{6,7},{9,8},{8,9},{1... | collective-permute-start | bytes 12582920 | tf_op jit(solution)/shard_map/ppermute | solution.py:91
  748.3 17.4 %copy-start.3 = (s32[6144]{0:T(1024)S(1)}, s32[6144]{0:T(1024)}, u32[]{:S(2)}) copy-start(s32[6144]{0:T(1024)} %copy-done.2) | copy-start | bytes 73732
  748.3 24.1 %copy-start.4 = (f32[768,8]{0,1:T(8,128)S(1)}, f32[768,8]{0,1:T(8,128)}, u32[]{:S(2)}) copy-start(f32[768,8]{0,1:T(8,128)} %param.9) | copy-start | bytes 73732
  763.5 148.3 %collective-permute-start.1 = (bf16[1,2,512,2048]{3,2,1,0:T(8,128)(2,1)}, bf16[1,2,512,2048]{3,2,1,0:T(8,128)(2,1)}, u32[]{:S(2)}, u32[]{:S(2)}) collective-permute-start(bf16[1,2,512,2048]{3,2,1,0:T(8,128)(2,1)} %convert_bitcast_fusion.2), channel_id=1, source_target_pairs={{20,0},{21,1},{22,2},{23,3},{4,4},{5,5},{6,6},{7,7},{8,8},{9,9},{1... | collective-permute-start | bytes 12582920 | tf_op jit(solution)/shard_map/ppermute | solution.py:90
  937.1 81.5 %copy-start.1 = (bf16[768,2048]{1,0:T(8,128)(2,1)S(1)}, bf16[768,2048]{1,0:T(8,128)(2,1)}, u32[]{:S(2)}) copy-start(bf16[768,2048]{1,0:T(8,128)(2,1)} %param.7) | copy-start | bytes 9437188
where the time goes:
time: 1030 us; the launch traced here: 1020 us
  waiting for transfers between devices  636 us (62%)
  local copies, waits for them, and re-layouts  161 us (16%)
  matrix products  122 us (12%)
  other arithmetic  64 us (6%)
  starting transfers between devices  34.8 us (3%)
    ppermute x1, waiting for transfers between devices, device_body(): recv_same = lax.ppermute(send_hot[0], GROUP_AXES, perm_same)  287 us
    all_to_all x1, waiting for transfers between devices, device_body(): recv_base = lax.all_to_all(send_base, GROUP_AXES, 0, 0, tiled=True)  210 us
    ppermute x1, waiting for transfers between devices, device_body(): ret_same = lax.ppermute(y_same, GROUP_AXES, back_same)  96.4 us
    dot_general x3, matrix products, expert_ffn(): jnp.einsum('sepf,efd->sepd', hidden, w_down, preferred_element_type=jnp.f...  75.1 us
    gather x1, local copies, waits for them, and re-layouts, device_body(): y_copy = y_rows[jnp.argsort(src_copy)].reshape(tok_dev, top_k, d_model)  58 us
    ppermute x1, waiting for transfers between devices, device_body(): ret_other = lax.ppermute(y_other, GROUP_AXES, back_other)  42.1 us
    gather x1, local copies, waits for them, and re-layouts, device_body(): sort_order[copy_layout(dst_chip, core_id, n_exp, exp_dev, n_core, base_ro...  34.3 us
    gather x1, local copies, waits for them, and re-layouts, device_body(): send_rows = tokens[src_copy // top_k]  30.9 us
  transfers between devices with their start and end apart: 6, of which 4 were waited for; matrix products, arithmetic and copies ran while one was open for 15% of the time, Pallas kernels for 0%

commit v1 on v0

v1 whole, which is shorter than its diff:
```python
import functools

import jax
import jax.numpy as jnp
from jax import lax
from jax.experimental import pallas as pl
from jax.experimental.pallas import tpu as pltpu
from jax.sharding import PartitionSpec as P

TOKEN_SPEC = P(('dp', 'ey', 'ex', 'core'), None)
EXPERT_SPEC = P(('ey', 'ex', 'core'), None, None)
F32 = jnp.float32
BF16 = jnp.bfloat16
VMEM_LIMIT = 62 * 1024 * 1024
MESH = pl.DeviceIdType.MESH
AXES = (('ex', 'ey'), ('ey', 'ex'))


def target_chips(grid_y, grid_x):
    half_y, half_x = grid_y // 2, grid_x // 2
    chip_list = []
    for chip_y in range(grid_y):
        for chip_x in range(grid_x):
            if chip_y == 0 and chip_x < half_x:
                chip_list.append(half_y * grid_x + chip_x + half_x)
            elif chip_y == half_y and chip_x >= half_x:
                chip_list.append(chip_x - half_x)
            else:
                chip_list.append(chip_y * grid_x + chip_x)
    return chip_list


def is_moved(iy, ix, n):
    half = n // 2
    return ((iy == 0) & (ix < half)) | ((iy == half) & (ix >= half))


def row_to_columns(row):
    return jnp.transpose(jnp.broadcast_to(row, (128, row.shape[1])))


def pick_matrix(row, n_tok):
    cols = row_to_columns(row)
    lane = lax.broadcasted_iota(jnp.int32, cols.shape, 1).astype(F32)
    blocks = [(cols == lane + (128.0 * k)).astype(F32).astype(BF16) for k in range(n_tok // 128)]
    return jnp.concatenate(blocks, axis=1)


def spread_matrix(row, n_tok):
    tok = lax.broadcasted_iota(jnp.int32, (n_tok, row.shape[1]), 0).astype(F32)
    return (tok == row).astype(F32).astype(BF16)


def scaled_rows(rows, gate_row):
    cols = row_to_columns(gate_row)
    reps = rows.shape[1] // 128
    return (rows.astype(F32) * jnp.concatenate([cols] * reps, axis=1)).astype(BF16)


def dot(a, b):
    return jnp.dot(a, b, preferred_element_type=F32)


class Here:
    def __init__(self, n, n_core):
        self.n, self.n_core = n, n_core
        self.iy, self.ix, self.ic = (lax.axis_index(a) for a in ('ey', 'ex', 'core'))
        self.at = {'ey': self.iy, 'ex': self.ix, 'core': self.ic}

    def step(self, axis, by):
        size = self.n_core if axis == 'core' else self.n
        return lax.rem(self.at[axis] + (by % size), size)

    def dev(self, **by):
        return {axis: self.step(axis, k) for axis, k in by.items()}

    def moved(self):
        return is_moved(self.iy, self.ix, self.n)

    def middle(self):
        return is_moved(self.iy, self.step('ex', self.n // 2), self.n)

    def barrier(self):
        sem = pltpu.get_barrier_semaphore()
        peers = [self.dev(**{axis: k, 'core': c}) for axis in ('ey', 'ex') for k in range(1, self.n) for c in range(self.n_core)]
        peers += [self.dev(core=1), self.dev(ey=self.n // 2, ex=self.n // 2)]
        for peer in peers:
            pl.semaphore_signal(sem, inc=1, device_id=peer, device_id_type=MESH)
        pl.semaphore_wait(sem, len(peers))


def remote(src, dst, send_sem, recv_sem, dev):
    return pltpu.make_async_remote_copy(src_ref=src, dst_ref=dst, send_sem=send_sem, recv_sem=recv_sem, device_id=dev, device_id_type=MESH)


def dispatch_kernel(n, n_core, tok_ref, tx_ref, ht_ref, rx_ref, htr_ref, r1_ref, r2_ref, hk_ref, hr_ref,
                    g_ref, hb_ref, sb_ref, hp_ref, own_sem, tab_s, tab_r, g_s, g_r, d_s, d_r, hot_s, hot_r, swap_s, swap_r, keep_sem):
    here = Here(n, n_core)
    tok_dev, d_model = tok_ref.shape
    dh = d_model // 2
    half = tok_dev // 2
    lo, hi = pl.ds(0, half), pl.ds(half, half)
    n_dst, n_src, base_rows, _ = sb_ref.shape[2:]
    exp_dev = sb_ref.shape[1]
    outs = (r1_ref, r2_ref)
    own = [pltpu.make_async_copy(tok_ref.at[:, pl.ds(h * dh, dh)], g_ref.at[h, 0], own_sem.at[h]) for h in range(2)]
    for c in own:
        c.start()
    here.barrier()

    tabs = []
    for h in range(2):
        rx_ref[h, 0] = tx_ref[h, 0]
        for k in range(1, n):
            c = remote(tx_ref.at[h, k], rx_ref.at[h, k], tab_s.at[h * n + k], tab_r.at[h * n + k], here.dev(**{AXES[h][0]: k}))
            c.start()
            tabs.append(c)
    moved = here.moved()
    middle = here.middle()
    hot_tab = remote(ht_ref, htr_ref, tab_s.at[0], tab_r.at[0], here.dev(ey=n // 2, ex=n // 2))

    @pl.when(moved)
    def _():
        hot_tab.start()

    @pl.when(jnp.logical_not(moved))
    def _():
        htr_ref[...] = ht_ref[...]

    first = []
    for h in range(2):
        own[h].wait()
        axis = AXES[h][0]
        for i, (slot, rows, by) in enumerate(((1, lo, 1), (3, hi, -1), (1, hi, 1), (3, lo, -1))):
            c = remote(g_ref.at[h, 0, rows], g_ref.at[h, slot, rows], g_s.at[h, i], g_r.at[h, i], here.dev(**{axis: by}))
            c.start()
            first.append(c)
    far = []
    for i, (slot, rows, by) in enumerate(((1, lo, 1), (3, hi, -1))):
        for h in range(2):
            first[h * 4 + i].wait_recv()
            c = remote(g_ref.at[h, slot, rows], g_ref.at[h, 2, rows], g_s.at[h, 4 + i], g_r.at[h, 4 + i], here.dev(**{AXES[h][0]: by}))
            c.start()
            far.append(c)
    for c in tabs:
        c.wait_recv()

    for h in range(2):
        first[h * 4 + 2].wait_recv()
        first[h * 4 + 3].wait_recv()
    for c in far:
        c.wait_recv()
    sends = []
    for e in range(exp_dev):
        for h in range(2):
            @pl.loop(0, n_src)
            def _(s):
                mat = pick_matrix(rx_ref[h, s, 2 * e:2 * e + 1], tok_dev)
                sb_ref[h, e, :, pl.ds(s, 1)] = dot(mat, g_ref[h, s]).astype(BF16).reshape(n_dst, 1, base_rows, dh)

            for j in range(n_dst - 1, 0, -1):
                c = remote(sb_ref.at[h, e, j], outs[h].at[e, j], d_s.at[h, e, j], d_r.at[h, e, j], here.dev(**{AXES[h][1]: j // n_core, 'core': j % n_core}))
                c.start()
                sends.append(c)
            c = pltpu.make_async_copy(sb_ref.at[h, e, 0], outs[h].at[e, 0], d_s.at[h, e, 0])
            c.start()
            sends.append(c)

    hot = [remote(g_ref.at[h, 2], hb_ref.at[h], hot_s.at[h], hot_r.at[h], here.dev(**{AXES[h][1]: n // 2})) for h in range(2)]

    @pl.when(middle)
    def _():
        for c in hot:
            c.start()

    @pl.when(jnp.logical_not(moved))
    def _():
        for h in range(2):
            hb_ref[h] = g_ref[h, 0]

    @pl.when(moved)
    def _():
        hot_tab.wait_recv()
        for c in hot:
            c.wait_recv()

    swap = []
    for rel in range(n_core - 1, -1, -1):
        @pl.loop(0, exp_dev)
        def _(e):
            mat = pick_matrix(htr_ref[pl.ds(rel * exp_dev + e, 1)], tok_dev)
            for h in range(2):
                hp_ref[rel, e, :, h * dh:(h + 1) * dh] = dot(mat, hb_ref[h]).astype(BF16)

        if rel:
            c = remote(hp_ref.at[rel], hr_ref, swap_s, swap_r, here.dev(core=rel))
        else:
            c = pltpu.make_async_copy(hp_ref.at[rel], hk_ref, keep_sem)
        c.start()
        swap.append(c)

    for c in swap + sends + tabs:
        c.wait() if not c.is_remote else c.wait_send()
    for c in first + far:
        c.wait_send()
    for c in sends:
        if c.is_remote:
            c.wait_recv()
    swap[0].wait_recv()

    @pl.when(moved)
    def _():
        hot_tab.wait_send()

    @pl.when(middle)
    def _():
        for c in hot:
            c.wait_send()


def dispatch(n, n_core, exp_dev, base_rows, hot_rows, tokens, tx, ht):
    tok_dev, d_model = tokens.shape
    dh = d_model // 2
    n_dst = n * n_core
    any_ = pl.BlockSpec(memory_space=pl.ANY)
    vm = pl.BlockSpec(memory_space=pltpu.VMEM)
    recv = jax.ShapeDtypeStruct((exp_dev, n_dst, n, base_rows, dh), BF16)
    hot = jax.ShapeDtypeStruct((exp_dev, hot_rows, d_model), BF16)
    dma = pltpu.SemaphoreType.DMA
    return pl.pallas_call(
        functools.partial(dispatch_kernel, n, n_core),
        out_shape=(jax.ShapeDtypeStruct(tx.shape, F32), jax.ShapeDtypeStruct(ht.shape, F32), recv, recv, hot, hot),
        in_specs=[any_, vm, vm],
        out_specs=(vm, vm, any_, any_, any_, any_),
        scratch_shapes=[
            pltpu.VMEM((2, n, tok_dev, dh), BF16),
            pltpu.VMEM((2, tok_dev, dh), BF16),
            pltpu.VMEM((2, exp_dev, n_dst, n, base_rows, dh), BF16),
            pltpu.VMEM((n_core, exp_dev, hot_rows, d_model), BF16),
            dma((2,)), dma((2 * n,)), dma((2 * n,)), dma((2, 6)), dma((2, 6)),
            dma((2, exp_dev, n_dst)), dma((2, exp_dev, n_dst)), dma((2,)), dma((2,)), dma, dma, dma,
        ],
        compiler_params=pltpu.CompilerParams(vmem_limit_bytes=VMEM_LIMIT, collective_id=0, has_side_effects=True),
        name='dispatch',
    )(tokens, tx, ht)


def return_kernel(n, n_core, rx_ref, htr_ref, y1e0, y2e0, y1e1, y2e1, hk_ref, hr_ref, out_ref,
                  q_ref, hy_ref, p_ref, s_ref, hs_ref, u_ref, w_ref, d_s, d_r, swap_s, swap_r, keep_sem, hot_s, hot_r, ring_s, ring_r):
    here = Here(n, n_core)
    tok_dev, d_model = out_ref.shape
    dh = d_model // 2
    half = tok_dev // 2
    lo, hi = pl.ds(0, half), pl.ds(half, half)
    exp_dev, n_dst, n_src, base_rows, _ = q_ref.shape[1:]
    ys = ((y1e0, y1e1), (y2e0, y2e1))
    keep = pltpu.make_async_copy(hk_ref, hy_ref.at[0], keep_sem)
    keep.start()
    here.barrier()
    sends = []
    for e in range(exp_dev):
        for h in range(2):
            for j in range(n_dst - 1, 0, -1):
                c = remote(ys[h][e].at[j], q_ref.at[h, e, j], d_s.at[h, e, j], d_r.at[h, e, j], here.dev(**{AXES[h][1]: -(j // n_core), 'core': j % n_core}))
                c.start()
                sends.append(c)
            c = pltpu.make_async_copy(ys[h][e].at[0], q_ref.at[h, e, 0], d_s.at[h, e, 0])
            c.start()
            sends.append(c)
        if e == 0:
            swap = remote(hr_ref, hy_ref.at[1], swap_s, swap_r, here.dev(core=1))
            swap.start()
    moved = here.moved()
    middle = here.middle()

    keep.wait()
    swap.wait_recv()
    for h in range(2):
        acc = None
        for k in range(n_core * exp_dev):
            rows = scaled_rows(hy_ref[k // exp_dev, k % exp_dev, :, h * dh:(h + 1) * dh], htr_ref[n_core * exp_dev + k:n_core * exp_dev + k + 1])
            term = dot(spread_matrix(htr_ref[k:k + 1], tok_dev), rows)
            acc = term if acc is None else acc + term
        s_ref[h] = acc.astype(BF16)
    hot = [remote(s_ref.at[h], hs_ref.at[h], hot_s.at[h], hot_r.at[h], here.dev(**{AXES[h][1]: n // 2})) for h in range(2)]

    @pl.when(moved)
    def _():
        for c in hot:
            c.start()

    for c in sends:
        if c.is_remote:
            c.wait_recv()
        else:
            c.wait()

    @pl.when(middle)
    def _():
        for c in hot:
            c.wait_recv()

    def spread(h, s):
        acc = None
        for e in range(exp_dev):
            rows = q_ref[h, e, :, s].reshape(n_dst * base_rows, dh)
            term = dot(spread_matrix(rx_ref[h, s, 2 * e:2 * e + 1], tok_dev), scaled_rows(rows, rx_ref[h, s, 2 * e + 1:2 * e + 2]))
            acc = term if acc is None else acc + term
        return acc

    ring = []

    def send(h, i, src, dst, by):
        c = remote(src, dst, ring_s.at[h, i], ring_r.at[h, i], here.dev(**{AXES[h][0]: by}))
        c.start()
        ring.append(c)
        return c

    ups, downs = [], []
    for h in range(2):
        p_ref[h, 2] = spread(h, 2).astype(BF16)

        @pl.when(middle)
        def _():
            p_ref[h, 2] = (p_ref[h, 2].astype(F32) + hs_ref[h].astype(F32)).astype(BF16)

        ups.append(send(h, 0, p_ref.at[h, 2, lo], u_ref.at[h, lo], 1))
        downs.append(send(h, 1, p_ref.at[h, 2, hi], u_ref.at[h, hi], -1))
    last = []
    for h in range(2):
        p_ref[h, 3] = spread(h, 3).astype(BF16)
        last.append(send(h, 2, p_ref.at[h, 3, hi], w_ref.at[h, 0, hi], 1))
        p_ref[h, 1] = spread(h, 1).astype(BF16)
        last.append(send(h, 3, p_ref.at[h, 1, lo], w_ref.at[h, 1, lo], -1))
    for h in range(2):
        ups[h].wait_recv()
        p_ref[h, 3, lo] = (p_ref[h, 3, lo].astype(F32) + u_ref[h, lo].astype(F32)).astype(BF16)
        last.append(send(h, 4, p_ref.at[h, 3, lo], w_ref.at[h, 0, lo], 1))
        downs[h].wait_recv()
        p_ref[h, 1, hi] = (p_ref[h, 1, hi].astype(F32) + u_ref[h, hi].astype(F32)).astype(BF16)
        last.append(send(h, 5, p_ref.at[h, 1, hi], w_ref.at[h, 1, hi], -1))
    own_hot = jnp.where(moved, 0.0, 1.0).astype(F32)
    for h in range(2):
        p_ref[h, 0] = (spread(h, 0) + own_hot * s_ref[h].astype(F32)).astype(BF16)
    for c in last:
        c.wait_recv()
    for h in range(2):
        out_ref[:, h * dh:(h + 1) * dh] = (p_ref[h, 0].astype(F32) + w_ref[h, 0].astype(F32) + w_ref[h, 1].astype(F32)).astype(BF16)

    for c in sends:
        if c.is_remote:
            c.wait_send()
    swap.wait_send()
    for c in ring:
        c.wait_send()

    @pl.when(moved)
    def _():
        for c in hot:
            c.wait_send()


def combine(n, n_core, tok_dev, rx, htr, ys, hk, hr):
    exp_dev, n_dst, n_src, base_rows, dh = 2, *ys[0].shape
    any_ = pl.BlockSpec(memory_space=pl.ANY)
    vm = pl.BlockSpec(memory_space=pltpu.VMEM)
    dma = pltpu.SemaphoreType.DMA
    half_tok = pltpu.VMEM((2, tok_dev, dh), BF16)
    return pl.pallas_call(
        functools.partial(return_kernel, n, n_core),
        out_shape=jax.ShapeDtypeStruct((tok_dev, 2 * dh), BF16),
        in_specs=[vm, vm] + [any_] * 6,
        out_specs=vm,
        scratch_shapes=[
            pltpu.VMEM((2, exp_dev, n_dst, n_src, base_rows, dh), BF16),
            pltpu.VMEM((n_core,) + hk.shape, BF16),
            pltpu.VMEM((2, n, tok_dev, dh), BF16),
            half_tok, half_tok, half_tok,
            pltpu.VMEM((2, 2, tok_dev, dh), BF16),
            dma((2, exp_dev, n_dst)), dma((2, exp_dev, n_dst)), dma, dma, dma, dma((2,)), dma((2,)), dma((2, 6)), dma((2, 6)),
        ],
        compiler_params=pltpu.CompilerParams(vmem_limit_bytes=VMEM_LIMIT, collective_id=1, has_side_effects=True),
        name='combine',
    )(rx, htr, *ys, hk, hr)


def gated_mlp(x, wg_ref, wu_ref, wd_ref):
    gate = dot(x, wg_ref[0])
    up = dot(x, wu_ref[0])
    hidden = (jax.nn.silu(gate) * up).astype(BF16)
    return dot(hidden, wd_ref[0]).astype(BF16)


def base_ffn_kernel(x1_ref, x2_ref, wg_ref, wu_ref, wd_ref, y1_ref, y2_ref):
    dh = x1_ref.shape[-1]
    n_core, n_col, base_rows = x1_ref.shape[2:5]
    for c in range(n_core):
        x1 = x1_ref[0, 0, c].reshape(n_col * base_rows, dh)
        x2 = x2_ref[0, :, c, 0].reshape(n_col * base_rows, dh)
        gate = dot(x1, wg_ref[0, :dh]) + dot(x2, wg_ref[0, dh:])
        up = dot(x1, wu_ref[0, :dh]) + dot(x2, wu_ref[0, dh:])
        hidden = (jax.nn.silu(gate) * up).astype(BF16)
        y1_ref[0, c] = dot(hidden, wd_ref[0, :, :dh]).astype(BF16).reshape(n_col, base_rows, dh)
        y2_ref[:, c, 0] = dot(hidden, wd_ref[0, :, dh:]).astype(BF16).reshape(n_col, base_rows, dh)


def base_ffn(e, r1, r2, w_gate, w_up, w_down):
    _, n, n_core, _, base_rows, dh = r1.shape
    _, d_model, d_ff = w_gate.shape
    ws = pl.BlockSpec((1, d_model, d_ff), lambda i: (e, 0, 0))
    wd = pl.BlockSpec((1, d_ff, d_model), lambda i: (e, 0, 0))
    out = jax.ShapeDtypeStruct((n, n_core, n, base_rows, dh), BF16)
    n_row = n * n_core * n * base_rows
    return pl.pallas_call(
        base_ffn_kernel,
        grid=(n,),
        out_shape=(out, out),
        in_specs=[
            pl.BlockSpec((1, 1, n_core, n, base_rows, dh), lambda i: (e, i, 0, 0, 0, 0)),
            pl.BlockSpec((1, n, n_core, 1, base_rows, dh), lambda i: (e, 0, 0, i, 0, 0)),
            ws, ws, wd,
        ],
        out_specs=(
            pl.BlockSpec((1, n_core, n, base_rows, dh), lambda i: (i, 0, 0, 0, 0)),
            pl.BlockSpec((n, n_core, 1, base_rows, dh), lambda i: (0, 0, i, 0, 0)),
        ),
        compiler_params=pltpu.CompilerParams(vmem_limit_bytes=VMEM_LIMIT),
        cost_estimate=pl.CostEstimate(flops=6 * n_row * d_model * d_ff, bytes_accessed=8 * n_row * d_model, transcendentals=n_row * d_ff),
        name='base_ffn',
    )(r1, r2, w_gate, w_up, w_down)


def hot_ffn_kernel(xa_ref, xb_ref, wg_ref, wu_ref, wd_ref, ya_ref, yb_ref):
    ya_ref[0] = gated_mlp(xa_ref[0], wg_ref, wu_ref, wd_ref)
    yb_ref[0] = gated_mlp(xb_ref[0], wg_ref, wu_ref, wd_ref)


def hot_ffn(xa, xb, w_gate, w_up, w_down):
    exp_dev, d_model, d_ff = w_gate.shape
    rows = xa.shape[1]
    spec = pl.BlockSpec((1, rows, d_model), lambda e: (e, 0, 0))
    ws = pl.BlockSpec((1, d_model, d_ff), lambda e: (e, 0, 0))
    wd = pl.BlockSpec((1, d_ff, d_model), lambda e: (e, 0, 0))
    n_row = 2 * exp_dev * rows
    return pl.pallas_call(
        hot_ffn_kernel,
        grid=(exp_dev,),
        out_shape=(jax.ShapeDtypeStruct(xa.shape, BF16),) * 2,
        in_specs=[spec, spec, ws, ws, wd],
        out_specs=(spec, spec),
        compiler_params=pltpu.CompilerParams(vmem_limit_bytes=VMEM_LIMIT),
        cost_estimate=pl.CostEstimate(flops=6 * n_row * d_model * d_ff, bytes_accessed=8 * n_row * d_model, transcendentals=n_row * d_ff),
        name='hot_ffn',
    )(xa, xb, w_gate, w_up, w_down)


def solution(mesh):
    grid_y = mesh.shape['ey']
    grid_x = mesh.shape['ex']
    n_core = mesh.shape['core']
    n = grid_x
    n_dev = grid_y * grid_x * n_core
    chip_list = target_chips(grid_y, grid_x)

    def device_body(tokens, expert_ids, gate_prob, w_gate, w_up, w_down):
        tok_dev, top_k = expert_ids.shape
        exp_dev = w_gate.shape[0]
        exp_chip = exp_dev * n_core
        n_exp = exp_dev * n_dev
        n_copy = tok_dev * top_k
        base_rows = 2 * n_copy // (3 * n_exp)
        hot_rows = grid_y * grid_x * base_rows // 2
        core = lax.axis_index('core')
        iy = lax.axis_index('ey')
        ix = lax.axis_index('ex')
        dst_chip = jnp.where(is_moved(iy, ix, n), lax.rem(iy + n // 2, n) * n + lax.rem(ix + n // 2, n), iy * n + ix)

        key = expert_ids.reshape(n_copy) * n_copy + jnp.arange(n_copy, dtype=jnp.int32)
        skey, sgate = lax.sort((key, gate_prob.reshape(n_copy)), num_keys=1, is_stable=False)
        stok = (lax.rem(skey, n_copy) // top_k).astype(F32)
        tab = jnp.stack([stok, sgate])
        lo = dst_chip * exp_chip
        hot_shift = hot_rows * exp_chip // base_rows
        by_block = tab.reshape(2, n_copy // base_rows, base_rows)
        e_id = jnp.arange(n_exp)[None, :, None]
        base = jnp.where(e_id < lo, by_block[:, :n_exp], by_block[:, hot_shift:hot_shift + n_exp])
        hot = lax.dynamic_slice(tab, (0, lo * base_rows), (2, exp_chip * (base_rows + hot_rows)))
        hot = hot.reshape(2, exp_chip, base_rows + hot_rows)
        base = lax.dynamic_update_slice(base, hot[:, :, :base_rows], (0, lo, 0))
        base = base.reshape(2, n, n, n_core, exp_dev, base_rows)
        base = lax.dynamic_slice_in_dim(jnp.concatenate([base, base], axis=1), iy, n, axis=1)
        base = lax.dynamic_slice_in_dim(jnp.concatenate([base, base], axis=2), ix, n, axis=2)
        base = jnp.where(core == 0, base, base[:, :, :, ::-1])
        hot = hot[:, :, base_rows:].reshape(2, n_core, exp_dev, hot_rows)
        hot = jnp.where(core == 0, hot, hot[:, ::-1])
        n_row = n * n_core * base_rows
        tx = jnp.stack([base.transpose(2, 4, 0, 1, 3, 5).reshape(n, exp_dev * 2, n_row), base.transpose(1, 4, 0, 2, 3, 5).reshape(n, exp_dev * 2, n_row)])
        tx = jnp.pad(tx, ((0, 0), (0, 0), (0, 8 - exp_dev * 2), (0, 0)))
        ht = hot.reshape(2 * exp_chip, hot_rows)

        rx, htr, r1, r2, hk, hr = dispatch(n, n_core, exp_dev, base_rows, hot_rows, tokens, tx, ht)
        r1 = r1.reshape(exp_dev, n, n_core, n, base_rows, -1)
        r2 = r2.reshape(exp_dev, n, n_core, n, base_rows, -1)
        ys = []
        for e in range(exp_dev):
            ys += [y.reshape(n * n_core, n, base_rows, -1) for y in base_ffn(e, r1, r2, w_gate, w_up, w_down)]
        yk, yr = hot_ffn(hk, hr, w_gate, w_up, w_down)
        return combine(n, n_core, tok_dev, rx, htr, ys, yk, yr)

    return jax.shard_map(device_body, mesh=mesh, in_specs=(TOKEN_SPEC, TOKEN_SPEC, TOKEN_SPEC, EXPERT_SPEC, EXPERT_SPEC, EXPERT_SPEC), out_specs=TOKEN_SPEC, check_vma=False)
```

time: 1030 us -> 519 us (0.50)
  the two profiles are of different devices: /device:TPU:98 before, /device:TPU:97 now
where the time goes in v1:
time: 519 us; the launch traced here: 511 us
  Pallas kernels  496 us (96%)
  other arithmetic  7.5 us (1%)
  local copies, waits for them, and re-layouts  6.72 us (1%)
    pallas_call x1, Pallas kernels, dispatch(): pl.pallas_call(functools.partial(dispatch_kernel, n, n_core), out_shape=(...  209 us
    pallas_call x1, Pallas kernels, combine(): pl.pallas_call(functools.partial(return_kernel, n, n_core), out_shape=jax...  187 us
    pallas_call x2, Pallas kernels, base_ffn(): pl.pallas_call(base_ffn_kernel, grid=(n,), out_shape=(out, out), in_specs...  66.2 us
    pallas_call x1, Pallas kernels, hot_ffn(): pl.pallas_call(hot_ffn_kernel, grid=(exp_dev,), out_shape=(jax.ShapeDtype...  33.9 us

profile of v1, /device:TPU:97, one launch (start us, length us, event | category | flops | bytes accessed | tf_op | source)
XLA Modules:
  0.0 511.1 jit_solution(5701158170389248625)
XLA Ops:
  0.0 0.7 broadcast_multiply_fusion
  0.7 0.2 copy.8
  0.9 0.2 mul.22
  1.1 0.9 copy.9
  2.0 0.2 reshape.46
  2.2 5.7 %sort.15 = (s32[6144]{0:T(1024)S(1)}, f32[6144]{0:T(1024)S(1)}) sort(s32[6144]{0:T(1024)S(1)} %iota_add_fusion, f32[6144]{0:T(1024)S(1)} %reshape.46), dimensions={0}, to_apply=%region_0.1 | sort | flops 79872 | bytes 98304 | tf_op jit(solution)/shard_map/sort | solution.py:479
  7.9 0.1 fusion.7
  8.1 0.1 reshape.47
  8.1 0.1 slice.19
  8.3 0.6 reshape.50.ht_ref
  8.9 0.1 stack.18
  9.0 0.1 stack.19
  9.0 0.1 slice_select_fusion
  9.1 0.1 fusion.1
  9.2 0.1 fusion
  9.4 0.1 stack_reshape.6
  9.6 0.1 stack_reshape.7
  9.7 0.7 select_maximum_fusion.tx_ref
  10.3 209.4 %dispatch.1 = (f32[2,4,8,512]{3,2,1,0:T(8,128)}, f32[8,512]{1,0:T(8,128)}, bf16[2,8,4,64,1024]{4,3,2,1,0:T(8,128)(2,1)}, bf16[2,8,4,64,1024]{4,3,2,1,0:T(8,128)(...) custom-call(bf16[768,2048]{1,0:T(8,128)(2,1)} %tok_ref.1, ...), custom_call_target="tpu_custom_call" | custom-call | tf_op jit(solution)/shard_map/dispatch/pallas_call | solution.py:230
  219.7 33.1 %base_ffn.3 = (bf16[4,2,4,64,1024]{4,3,2,1,0:T(8,128)(2,1)}, bf16[4,2,4,64,1024]{4,3,2,1,0:T(8,128)(2,1)}) custom-call(bf16[2,4,2,4,64,1024]{5,4,3,2,1,0:T(8,128)(2,1)} %bitcast.20, bf16[2,4,2,4,64,1024]{5,4,3,2,1,0:T(8,128)(2,1)} %bitcast.22, bf16[2,2048,1024]{2,1,0:T(8,128)(2,1)} %wg_ref.5, bf16[2,2048,1024]{2,1,0:T(8,128)(2,1)} %wu_ref.5, ...), custom_call_target="tpu_custom_call" | custom-call | flops 25769803776 | bytes 33554432 | tf_op jit(solution)/shard_map/base_ffn/pallas_call | solution.py:414
  252.8 33.1 %base_ffn.2 = (bf16[4,2,4,64,1024]{4,3,2,1,0:T(8,128)(2,1)}, bf16[4,2,4,64,1024]{4,3,2,1,0:T(8,128)(2,1)}) custom-call(bf16[2,4,2,4,64,1024]{5,4,3,2,1,0:T(8,128)(2,1)} %bitcast.21, bf16[2,4,2,4,64,1024]{5,4,3,2,1,0:T(8,128)(2,1)} %bitcast.23, bf16[2,2048,1024]{2,1,0:T(8,128)(2,1)} %wg_ref.5, bf16[2,2048,1024]{2,1,0:T(8,128)(2,1)} %wu_ref.5, ...), custom_call_target="tpu_custom_call" | custom-call | flops 25769803776 | bytes 33554432 | tf_op jit(solution)/shard_map/base_ffn/pallas_call | solution.py:414
  286.0 33.9 %hot_ffn.1 = (bf16[2,512,2048]{2,1,0:T(8,128)(2,1)}, bf16[2,512,2048]{2,1,0:T(8,128)(2,1)}) custom-call(bf16[2,512,2048]{2,1,0:T(8,128)(2,1)} %get-tuple-element.29.xa_ref, bf16[2,512,2048]{2,1,0:T(8,128)(2,1)} %get-tuple-element.30.xb_ref, bf16[2,2048,1024]{2,1,0:T(8,128)(2,1)} %wg_ref.5, bf16[2,2048,1024]{2,1,0:T(8,128)(2,1)} %wu_ref.5, ...), custom_call_target="tpu_custom_call" | custom-call | flops 25769803776 | bytes 33554432 | tf_op jit(solution)/shard_map/hot_ffn/pallas_call | solution.py:445
  319.9 186.8 %combine.1 = bf16[768,2048]{1,0:T(8,128)(2,1)} custom-call(f32[2,4,8,512]{3,2,1,0:T(8,128)} %get-tuple-element.21.rx_ref, f32[8,512]{1,0:T(8,128)} %get-tuple-element.22.htr_ref, bf16[8,4,64,1024]{3,2,1,0:T(8,128)(2,1)} %bitcast.15, bf16[8,4,64,1024]{3,2,1,0:T(8,128)(2,1)} %bitcast.16, bf16[8,4,64,1024]{3,2,1,0:T(8,128)(2,1)} %bitcast.13, ...), custom_call_target="tpu_custom_call" | custom-call | tf_op jit(solution)/shard_map/combine/pallas_call | solution.py:369
  506.7 4.0 copy.15
  (11 shorter events, 0.2 us)
